TPU v7x, 32 devices: a 4x4x1 block of a 4x4x8 slice. The times are simulated.
32 devices in a mesh: dp: 1 (over z), cp: 32 (over y, x, core).
Axes of the slice: x: 4, y: 4, z: 1, core: 2. Of those that a mesh axis runs over, the one named last changes fastest.
The devices are a block of a 4x4x8 slice.
Arguments:
- x: bfloat16 [8192, 3072], P(('dp', 'cp'))
- seg: int32 [8192], P(('dp', 'cp'))
- wq: bfloat16 [3072, 3072], replicated
- wk: bfloat16 [3072, 1024], replicated
- wv: bfloat16 [3072, 1024], replicated
- wo: bfloat16 [3072, 3072], replicated
Outputs:
- output: bfloat16 [8192, 3072], P(('dp', 'cp'))
All inputs are finite; a program needn't handle non-finite values.
Results may differ from a plain program's by a relative error of at most 0.00598599.
Values are sent between devices in bfloat16 or wider.
A program may use at most 768 MiB of HBM per device.

v0:
```python
import jax
import jax.numpy as jnp
from jax import lax
from jax.sharding import PartitionSpec as P

DH = 128


def _positions(src, n, half):
    ar = jnp.arange(half, dtype=jnp.int32)
    return jnp.concatenate([src * half + ar, (2 * n - 1 - src) * half + ar])


def _block(q, k, v, mask, m, l, acc):
    s = jnp.einsum("qhgd,khd->hgqk", q, k, preferred_element_type=jnp.float32) * (DH ** -0.5)
    s = jnp.where(mask, s, -jnp.inf)
    m_new = jnp.maximum(m, s.max(axis=-1))
    m_safe = jnp.where(jnp.isfinite(m_new), m_new, 0.0)
    p = jnp.exp(s - m_safe[..., None])
    corr = jnp.exp(m - m_safe)
    l = l * corr + p.sum(axis=-1)
    pv = jnp.einsum("hgqk,khd->qhgd", p.astype(jnp.bfloat16), v, preferred_element_type=jnp.float32)
    acc = acc * jnp.transpose(corr, (2, 0, 1))[..., None] + pv
    return m_new, l, acc


def _finish(l, acc, wo):
    o = (acc / jnp.transpose(l, (2, 0, 1))[..., None]).astype(jnp.bfloat16)
    o = o.reshape(o.shape[0], -1)
    return jnp.dot(o, wo, preferred_element_type=jnp.float32).astype(jnp.bfloat16)


def solution(mesh):
    n = mesh.shape["cp"]
    perm = [(j, (j + 1) % n) for j in range(n)]

    def local(x, seg, wq, wk, wv, wo):
        lq = x.shape[0]
        half = lq // 2
        hq = wq.shape[1] // DH
        hkvv = wk.shape[1] // DH
        g = hq // hkvv
        me = lax.axis_index("cp")
        pos = _positions(me, n, half)
        q = jnp.dot(x, wq, preferred_element_type=jnp.float32).astype(jnp.bfloat16).reshape(lq, hkvv, g, DH)
        k = jnp.dot(x, wk, preferred_element_type=jnp.float32).astype(jnp.bfloat16).reshape(lq, hkvv, DH)
        v = jnp.dot(x, wv, preferred_element_type=jnp.float32).astype(jnp.bfloat16).reshape(lq, hkvv, DH)
        m = jnp.full((hkvv, g, lq), -jnp.inf, jnp.float32)
        l = jnp.zeros((hkvv, g, lq), jnp.float32)
        acc = jnp.zeros((lq, hkvv, g, DH), jnp.float32)
        kb, vb, sb = k, v, seg
        for step in range(n):
            if step > 0:
                kb = lax.ppermute(kb, "cp", perm)
                vb = lax.ppermute(vb, "cp", perm)
                sb = lax.ppermute(sb, "cp", perm)
            src = (me - step) % n
            mask = (seg[:, None] == sb[None, :]) & (_positions(src, n, half)[None, :] <= pos[:, None])
            m, l, acc = _block(q, kb, vb, mask, m, l, acc)
        return _finish(l, acc, wo)

    rows = P(("dp", "cp"), None)
    return jax.shard_map(local, mesh=mesh, in_specs=(rows, P(("dp", "cp")), P(), P(), P(), P()), out_specs=rows, check_vma=False)
```

profile of v0, /device:TPU:96, one launch (start us, length us, event | category | flops | bytes accessed | tf_op | source)
XLA Modules:
  0.0 792.9 jit_solution(5091073994833582456)
XLA Ops:
  11.7 10.4 %convolution_convert_fusion.1 = bf16[256,3072]{1,0:T(8,128)(2,1)} fusion(bf16[256,3072]{1,0:T(8,128)(2,1)S(1)} %copy-done, bf16[3072,3072]{1,0:T(8,128)(2,1)} %param.8), kind=kOutput, calls=%fused_computation.161 | convolution fusion | flops 4832624640 | bytes 22020096 | tf_op jit(solution)/shard_map/dot_general | solution.py:45
  26.1 8.3 %collective-permute-done.4 = bf16[256,8,128]{2,0,1:T(8,128)(2,1)S(1)} collective-permute-done((bf16[256,8,128]{2,0,1:T(8,128)(2,1)}, bf16[256,8,128]{2,0,1:T(8,128)(2,1)S(1)}, u32[]{:S(2)}, u32[]{:S(2)}) %collective-permute-start.4) | collective-permute-done | bytes 524320 | tf_op jit(solution)/shard_map/ppermute | solution.py:54
  40.1 6.3 collective-permute-done.7
  52.0 6.3 collective-permute-done.10
  63.9 6.3 collective-permute-done.3
  70.2 6.3 collective-permute-done.6
  76.6 6.3 collective-permute-done.9
  82.9 6.3 collective-permute-done.12
  89.2 6.3 collective-permute-done.15
  101.9 6.3 collective-permute-done.21
  108.2 6.3 collective-permute-done.24
  114.5 6.3 collective-permute-done.27
  120.8 6.3 collective-permute-done.30
  127.2 6.3 collective-permute-done.33
  133.5 6.3 collective-permute-done.36
  139.8 6.3 collective-permute-done.39
  146.1 6.3 collective-permute-done.42
  152.4 6.3 collective-permute-done.45
  158.8 6.3 collective-permute-done.48
  165.1 6.3 collective-permute-done.51
  171.4 6.3 collective-permute-done.54
  177.7 6.3 collective-permute-done.57
  184.0 6.3 collective-permute-done.60
  197.2 6.3 collective-permute-done.66
  203.6 6.3 collective-permute-done.69
  209.8 6.3 collective-permute-done.72
  609.3 6.2 fusion.126
  633.8 6.3 fusion.132
  670.7 6.3 fusion.140
  683.1 6.5 fusion.142
  748.6 33.5 %fusion.161 = bf16[256,8,3,128]{0,3,2,1:T(8,128)(2,1)S(1)} fusion(f32[8,128,3,256]{3,1,2,0:T(8,128)} %fusion.98, f32[8,128,3,256]{3,1,2,0:T(8,128)} %fusion.100, f32[8,128,3,256]{3,1,2,0:T(8,128)} %fusion.102, f32[8,128,3,256]{3,1,2,0:T(8,128)} %fusion.104, f32[8,128,3,256]{3,1,2,0:T(8,128)} %fusion.106, f32[8,128,3,256]{3,1,2,0:T(8,128)} %fusion.108, ...), kind=kOutput, calls=%fused_computation.196 | convolution fusion | flops 460062720 | bytes 106807296 | tf_op jit(solution)/shard_map/hgqk,khd->qhgd/dot_general | solution.py:22
  782.2 10.5 %convolution_convert_fusion = bf16[256,3072]{1,0:T(8,128)(2,1)} fusion(bf16[256,3072]{0,1:T(8,128)(2,1)S(1)} %bitcast.1381, bf16[3072,3072]{1,0:T(8,128)(2,1)} %param.11), kind=kOutput, calls=%fused_computation.160 | convolution fusion | flops 4832624640 | bytes 22020096 | tf_op jit(solution)/shard_map/dot_general | solution.py:30
  (607 shorter events, 551.7 us)
Async XLA Ops:
  0.0 58.3 %collective-permute-start = (s32[256]{0:T(256)}, s32[256]{0:T(256)S(1)}, u32[]{:S(2)}, u32[]{:S(2)}) collective-permute-start(s32[256]{0:T(256)} %param.7), channel_id=1, source_target_pairs={{0,1},{1,2},{2,3},{3,4},{4,5},{5,6},{6,7},{7,8},{8,9},{9,10},{10,1... | collective-permute-start | bytes 3080 | tf_op jit(solution)/shard_map/ppermute | solution.py:56
  7.5 14.9 %collective-permute-start.1 = (bf16[256,8,128]{2,0,1:T(8,128)(2,1)}, bf16[256,8,128]{2,0,1:T(8,128)(2,1)}, u32[]{:S(2)}, u32[]{:S(2)}) collective-permute-start(bf16[256,8,128]{2,0,1:T(8,128)(2,1)} %copy_bitcast_fusion), channel_id=1, source_target_pairs={{0,1},{1,2},{2,3},{3,4},{4,5},{5,6},{6,7},{7,8},{8,9},{9,10},{10,1... | collective-permute-start | bytes 1572872 | tf_op jit(solution)/shard_map/ppermute | solution.py:54
  10.6 15.5 %collective-permute-start.2 = (bf16[256,8,128]{0,2,1:T(8,128)(2,1)}, bf16[256,8,128]{0,2,1:T(8,128)(2,1)S(1)}, u32[]{:S(2)}, u32[]{:S(2)}) collective-permute-start(bf16[256,8,128]{0,2,1:T(8,128)(2,1)} %copy.82), channel_id=1, source_target_pairs={{0,1},{1,2},{2,3},{3,4},{4,5},{5,6},{6,7},{7,8},{8,9},{9,10},{10,1... | collective-permute-start | bytes 1572872 | tf_op jit(solution)/shard_map/ppermute | solution.py:55
  22.4 12.0 %collective-permute-start.4 = (bf16[256,8,128]{2,0,1:T(8,128)(2,1)}, bf16[256,8,128]{2,0,1:T(8,128)(2,1)S(1)}, u32[]{:S(2)}, u32[]{:S(2)}) collective-permute-start(bf16[256,8,128]{2,0,1:T(8,128)(2,1)} %collective-permute-done.1), channel_id=1, source_target_pairs={{0,1},{1,2},{2,3},{3,4},{4,5},{5,6},{6,7},{7,8},{8,9},{9,10},{10,1... | collective-permute-start | bytes 1572872 | tf_op jit(solution)/shard_map/ppermute | solution.py:54
  26.1 13.9 %collective-permute-start.5 = (bf16[256,8,128]{0,2,1:T(8,128)(2,1)S(1)}, bf16[256,8,128]{0,2,1:T(8,128)(2,1)S(1)}, u32[]{:S(2)}, u32[]{:S(2)}) collective-permute-start(bf16[256,8,128]{0,2,1:T(8,128)(2,1)S(1)} %collective-permute-done.2), channel_id=1, source_target_pairs={{0,1},{1,2},{2,3},{3,4},{4,5},{5,6},{6,7},{7,8},{8,9},{9,10},{10,1... | collective-permute-start | bytes 1572872 | tf_op jit(solution)/shard_map/ppermute | solution.py:55
  34.4 11.9 %collective-permute-start.7 = (bf16[256,8,128]{2,0,1:T(8,128)(2,1)S(1)}, bf16[256,8,128]{2,0,1:T(8,128)(2,1)S(1)}, u32[]{:S(2)}, u32[]{:S(2)}) collective-permute-start(bf16[256,8,128]{2,0,1:T(8,128)(2,1)S(1)} %collective-permute-done.4), channel_id=1, source_target_pairs={{0,1},{1,2},{2,3},{3,4},{4,5},{5,6},{6,7},{7,8},{8,9},{9,10},{10,1... | collective-permute-start | bytes 1572872 | tf_op jit(solution)/shard_map/ppermute | solution.py:54
  40.0 11.9 %collective-permute-start.8 = (bf16[256,8,128]{0,2,1:T(8,128)(2,1)S(1)}, bf16[256,8,128]{0,2,1:T(8,128)(2,1)S(1)}, u32[]{:S(2)}, u32[]{:S(2)}) collective-permute-start(bf16[256,8,128]{0,2,1:T(8,128)(2,1)S(1)} %collective-permute-done.5), channel_id=1, source_target_pairs={{0,1},{1,2},{2,3},{3,4},{4,5},{5,6},{6,7},{7,8},{8,9},{9,10},{10,1... | collective-permute-start | bytes 1572872 | tf_op jit(solution)/shard_map/ppermute | solution.py:55
  52.0 11.9 %collective-permute-start.11 = (bf16[256,8,128]{0,2,1:T(8,128)(2,1)S(1)}, bf16[256,8,128]{0,2,1:T(8,128)(2,1)S(1)}, u32[]{:S(2)}, u32[]{:S(2)}) collective-permute-start(bf16[256,8,128]{0,2,1:T(8,128)(2,1)S(1)} %collective-permute-done.8), channel_id=1, source_target_pairs={{0,1},{1,2},{2,3},{3,4},{4,5},{5,6},{6,7},{7,8},{8,9},{9,10},{10,1... | collective-permute-start | bytes 1572872 | tf_op jit(solution)/shard_map/ppermute | solution.py:55
  58.3 18.3 %collective-permute-start.13 = (bf16[256,8,128]{2,0,1:T(8,128)(2,1)}, bf16[256,8,128]{2,0,1:T(8,128)(2,1)}, u32[]{:S(2)}, u32[]{:S(2)}) collective-permute-start(bf16[256,8,128]{2,0,1:T(8,128)(2,1)} %collective-permute-done.10), channel_id=1, source_target_pairs={{0,1},{1,2},{2,3},{3,4},{4,5},{5,6},{6,7},{7,8},{8,9},{9,10},{10,1... | collective-permute-start | bytes 1572872 | tf_op jit(solution)/shard_map/ppermute | solution.py:54
  63.9 31.6 %collective-permute-start.14 = (bf16[256,8,128]{0,2,1:T(8,128)(2,1)S(1)}, bf16[256,8,128]{0,2,1:T(8,128)(2,1)S(1)}, u32[]{:S(2)}, u32[]{:S(2)}) collective-permute-start(bf16[256,8,128]{0,2,1:T(8,128)(2,1)S(1)} %collective-permute-done.11), channel_id=1, source_target_pairs={{0,1},{1,2},{2,3},{3,4},{4,5},{5,6},{6,7},{7,8},{8,9},{9,10},{10,1... | collective-permute-start | bytes 1572872 | tf_op jit(solution)/shard_map/ppermute | solution.py:55
  76.5 31.6 %collective-permute-start.16 = (bf16[256,8,128]{2,0,1:T(8,128)(2,1)}, bf16[256,8,128]{2,0,1:T(8,128)(2,1)}, u32[]{:S(2)}, u32[]{:S(2)}) collective-permute-start(bf16[256,8,128]{2,0,1:T(8,128)(2,1)} %collective-permute-done.13), channel_id=1, source_target_pairs={{0,1},{1,2},{2,3},{3,4},{4,5},{5,6},{6,7},{7,8},{8,9},{9,10},{10,1... | collective-permute-start | bytes 1572872 | tf_op jit(solution)/shard_map/ppermute | solution.py:54
  95.5 31.6 %collective-permute-start.17 = (bf16[256,8,128]{0,2,1:T(8,128)(2,1)S(1)}, bf16[256,8,128]{0,2,1:T(8,128)(2,1)}, u32[]{:S(2)}, u32[]{:S(2)}) collective-permute-start(bf16[256,8,128]{0,2,1:T(8,128)(2,1)S(1)} %collective-permute-done.14), channel_id=1, source_target_pairs={{0,1},{1,2},{2,3},{3,4},{4,5},{5,6},{6,7},{7,8},{8,9},{9,10},{10,1... | collective-permute-start | bytes 1572872 | tf_op jit(solution)/shard_map/ppermute | solution.py:55
  108.2 31.6 %collective-permute-start.19 = (bf16[256,8,128]{2,0,1:T(8,128)(2,1)}, bf16[256,8,128]{2,0,1:T(8,128)(2,1)}, u32[]{:S(2)}, u32[]{:S(2)}) collective-permute-start(bf16[256,8,128]{2,0,1:T(8,128)(2,1)} %collective-permute-done.16), channel_id=1, source_target_pairs={{0,1},{1,2},{2,3},{3,4},{4,5},{5,6},{6,7},{7,8},{8,9},{9,10},{10,1... | collective-permute-start | bytes 1572872 | tf_op jit(solution)/shard_map/ppermute | solution.py:54
  127.1 31.6 %collective-permute-start.20 = (bf16[256,8,128]{0,2,1:T(8,128)(2,1)}, bf16[256,8,128]{0,2,1:T(8,128)(2,1)}, u32[]{:S(2)}, u32[]{:S(2)}) collective-permute-start(bf16[256,8,128]{0,2,1:T(8,128)(2,1)} %collective-permute-done.17), channel_id=1, source_target_pairs={{0,1},{1,2},{2,3},{3,4},{4,5},{5,6},{6,7},{7,8},{8,9},{9,10},{10,1... | collective-permute-start | bytes 1572872 | tf_op jit(solution)/shard_map/ppermute | solution.py:55
  139.8 31.6 %collective-permute-start.22 = (bf16[256,8,128]{2,0,1:T(8,128)(2,1)}, bf16[256,8,128]{2,0,1:T(8,128)(2,1)}, u32[]{:S(2)}, u32[]{:S(2)}) collective-permute-start(bf16[256,8,128]{2,0,1:T(8,128)(2,1)} %collective-permute-done.19), channel_id=1, source_target_pairs={{0,1},{1,2},{2,3},{3,4},{4,5},{5,6},{6,7},{7,8},{8,9},{9,10},{10,1... | collective-permute-start | bytes 1572872 | tf_op jit(solution)/shard_map/ppermute | solution.py:54
  158.7 32.1 %collective-permute-start.23 = (bf16[256,8,128]{0,2,1:T(8,128)(2,1)}, bf16[256,8,128]{0,2,1:T(8,128)(2,1)}, u32[]{:S(2)}, u32[]{:S(2)}) collective-permute-start(bf16[256,8,128]{0,2,1:T(8,128)(2,1)} %collective-permute-done.20), channel_id=1, source_target_pairs={{0,1},{1,2},{2,3},{3,4},{4,5},{5,6},{6,7},{7,8},{8,9},{9,10},{10,1... | collective-permute-start | bytes 1572872 | tf_op jit(solution)/shard_map/ppermute | solution.py:55
  171.4 32.1 %collective-permute-start.25 = (bf16[256,8,128]{2,0,1:T(8,128)(2,1)}, bf16[256,8,128]{2,0,1:T(8,128)(2,1)}, u32[]{:S(2)}, u32[]{:S(2)}) collective-permute-start(bf16[256,8,128]{2,0,1:T(8,128)(2,1)} %collective-permute-done.22), channel_id=1, source_target_pairs={{0,1},{1,2},{2,3},{3,4},{4,5},{5,6},{6,7},{7,8},{8,9},{9,10},{10,1... | collective-permute-start | bytes 1572872 | tf_op jit(solution)/shard_map/ppermute | solution.py:54
  190.9 31.6 %collective-permute-start.26 = (bf16[256,8,128]{0,2,1:T(8,128)(2,1)}, bf16[256,8,128]{0,2,1:T(8,128)(2,1)}, u32[]{:S(2)}, u32[]{:S(2)}) collective-permute-start(bf16[256,8,128]{0,2,1:T(8,128)(2,1)} %collective-permute-done.23), channel_id=1, source_target_pairs={{0,1},{1,2},{2,3},{3,4},{4,5},{5,6},{6,7},{7,8},{8,9},{9,10},{10,1... | collective-permute-start | bytes 1572872 | tf_op jit(solution)/shard_map/ppermute | solution.py:55
  203.5 25.3 %collective-permute-start.28 = (bf16[256,8,128]{2,0,1:T(8,128)(2,1)}, bf16[256,8,128]{2,0,1:T(8,128)(2,1)}, u32[]{:S(2)}, u32[]{:S(2)}) collective-permute-start(bf16[256,8,128]{2,0,1:T(8,128)(2,1)} %collective-permute-done.25), channel_id=1, source_target_pairs={{0,1},{1,2},{2,3},{3,4},{4,5},{5,6},{6,7},{7,8},{8,9},{9,10},{10,1... | collective-permute-start | bytes 1572872 | tf_op jit(solution)/shard_map/ppermute | solution.py:54
  222.5 12.6 %collective-permute-start.29 = (bf16[256,8,128]{0,2,1:T(8,128)(2,1)}, bf16[256,8,128]{0,2,1:T(8,128)(2,1)S(1)}, u32[]{:S(2)}, u32[]{:S(2)}) collective-permute-start(bf16[256,8,128]{0,2,1:T(8,128)(2,1)} %collective-permute-done.26), channel_id=1, source_target_pairs={{0,1},{1,2},{2,3},{3,4},{4,5},{5,6},{6,7},{7,8},{8,9},{9,10},{10,1... | collective-permute-start | bytes 1572872 | tf_op jit(solution)/shard_map/ppermute | solution.py:55
  228.8 12.6 %collective-permute-start.31 = (bf16[256,8,128]{2,0,1:T(8,128)(2,1)}, bf16[256,8,128]{2,0,1:T(8,128)(2,1)S(1)}, u32[]{:S(2)}, u32[]{:S(2)}) collective-permute-start(bf16[256,8,128]{2,0,1:T(8,128)(2,1)} %collective-permute-done.28), channel_id=1, source_target_pairs={{0,1},{1,2},{2,3},{3,4},{4,5},{5,6},{6,7},{7,8},{8,9},{9,10},{10,1... | collective-permute-start | bytes 1572872 | tf_op jit(solution)/shard_map/ppermute | solution.py:54
  235.1 13.4 %collective-permute-start.32 = (bf16[256,8,128]{0,2,1:T(8,128)(2,1)S(1)}, bf16[256,8,128]{0,2,1:T(8,128)(2,1)S(1)}, u32[]{:S(2)}, u32[]{:S(2)}) collective-permute-start(bf16[256,8,128]{0,2,1:T(8,128)(2,1)S(1)} %collective-permute-done.29), channel_id=1, source_target_pairs={{0,1},{1,2},{2,3},{3,4},{4,5},{5,6},{6,7},{7,8},{8,9},{9,10},{10,1... | collective-permute-start | bytes 1572872 | tf_op jit(solution)/shard_map/ppermute | solution.py:55
  241.4 13.3 %collective-permute-start.34 = (bf16[256,8,128]{2,0,1:T(8,128)(2,1)S(1)}, bf16[256,8,128]{2,0,1:T(8,128)(2,1)S(1)}, u32[]{:S(2)}, u32[]{:S(2)}) collective-permute-start(bf16[256,8,128]{2,0,1:T(8,128)(2,1)S(1)} %collective-permute-done.31), channel_id=1, source_target_pairs={{0,1},{1,2},{2,3},{3,4},{4,5},{5,6},{6,7},{7,8},{8,9},{9,10},{10,1... | collective-permute-start | bytes 1572872 | tf_op jit(solution)/shard_map/ppermute | solution.py:54
  248.5 12.0 %collective-permute-start.35 = (bf16[256,8,128]{0,2,1:T(8,128)(2,1)S(1)}, bf16[256,8,128]{0,2,1:T(8,128)(2,1)S(1)}, u32[]{:S(2)}, u32[]{:S(2)}) collective-permute-start(bf16[256,8,128]{0,2,1:T(8,128)(2,1)S(1)} %collective-permute-done.32), channel_id=1, source_target_pairs={{0,1},{1,2},{2,3},{3,4},{4,5},{5,6},{6,7},{7,8},{8,9},{9,10},{10,1... | collective-permute-start | bytes 1572872 | tf_op jit(solution)/shard_map/ppermute | solution.py:55
  254.8 12.0 %collective-permute-start.37 = (bf16[256,8,128]{2,0,1:T(8,128)(2,1)S(1)}, bf16[256,8,128]{2,0,1:T(8,128)(2,1)S(1)}, u32[]{:S(2)}, u32[]{:S(2)}) collective-permute-start(bf16[256,8,128]{2,0,1:T(8,128)(2,1)S(1)} %collective-permute-done.34), channel_id=1, source_target_pairs={{0,1},{1,2},{2,3},{3,4},{4,5},{5,6},{6,7},{7,8},{8,9},{9,10},{10,1... | collective-permute-start | bytes 1572872 | tf_op jit(solution)/shard_map/ppermute | solution.py:54
  266.8 11.9 %collective-permute-start.40 = (bf16[256,8,128]{2,0,1:T(8,128)(2,1)S(1)}, bf16[256,8,128]{2,0,1:T(8,128)(2,1)S(1)}, u32[]{:S(2)}, u32[]{:S(2)}) collective-permute-start(bf16[256,8,128]{2,0,1:T(8,128)(2,1)S(1)} %collective-permute-done.37), channel_id=1, source_target_pairs={{0,1},{1,2},{2,3},{3,4},{4,5},{5,6},{6,7},{7,8},{8,9},{9,10},{10,1... | collective-permute-start | bytes 1572872 | tf_op jit(solution)/shard_map/ppermute | solution.py:54
  284.4 12.1 %collective-permute-start.44 = (bf16[256,8,128]{0,2,1:T(8,128)(2,1)S(1)}, bf16[256,8,128]{0,2,1:T(8,128)(2,1)S(1)}, u32[]{:S(2)}, u32[]{:S(2)}) collective-permute-start(bf16[256,8,128]{0,2,1:T(8,128)(2,1)S(1)} %collective-permute-done.41), channel_id=1, source_target_pairs={{0,1},{1,2},{2,3},{3,4},{4,5},{5,6},{6,7},{7,8},{8,9},{9,10},{10,1... | collective-permute-start | bytes 1572872 | tf_op jit(solution)/shard_map/ppermute | solution.py:55
  338.4 12.3 %collective-permute-start.58 = (bf16[256,8,128]{2,0,1:T(8,128)(2,1)S(1)}, bf16[256,8,128]{2,0,1:T(8,128)(2,1)S(1)}, u32[]{:S(2)}, u32[]{:S(2)}) collective-permute-start(bf16[256,8,128]{2,0,1:T(8,128)(2,1)S(1)} %collective-permute-done.55), channel_id=1, source_target_pairs={{0,1},{1,2},{2,3},{3,4},{4,5},{5,6},{6,7},{7,8},{8,9},{9,10},{10,1... | collective-permute-start | bytes 1572872 | tf_op jit(solution)/shard_map/ppermute | solution.py:54
  344.2 12.1 %collective-permute-start.59 = (bf16[256,8,128]{0,2,1:T(8,128)(2,1)S(1)}, bf16[256,8,128]{0,2,1:T(8,128)(2,1)S(1)}, u32[]{:S(2)}, u32[]{:S(2)}) collective-permute-start(bf16[256,8,128]{0,2,1:T(8,128)(2,1)S(1)} %collective-permute-done.56), channel_id=1, source_target_pairs={{0,1},{1,2},{2,3},{3,4},{4,5},{5,6},{6,7},{7,8},{8,9},{9,10},{10,1... | collective-permute-start | bytes 1572872 | tf_op jit(solution)/shard_map/ppermute | solution.py:55
  398.4 12.1 %collective-permute-start.73 = (bf16[256,8,128]{2,0,1:T(8,128)(2,1)S(1)}, bf16[256,8,128]{2,0,1:T(8,128)(2,1)S(1)}, u32[]{:S(2)}, u32[]{:S(2)}) collective-permute-start(bf16[256,8,128]{2,0,1:T(8,128)(2,1)S(1)} %collective-permute-done.70), channel_id=1, source_target_pairs={{0,1},{1,2},{2,3},{3,4},{4,5},{5,6},{6,7},{7,8},{8,9},{9,10},{10,1... | collective-permute-start | bytes 1572872 | tf_op jit(solution)/shard_map/ppermute | solution.py:54
  404.0 12.1 %collective-permute-start.74 = (bf16[256,8,128]{0,2,1:T(8,128)(2,1)S(1)}, bf16[256,8,128]{0,2,1:T(8,128)(2,1)S(1)}, u32[]{:S(2)}, u32[]{:S(2)}) collective-permute-start(bf16[256,8,128]{0,2,1:T(8,128)(2,1)S(1)} %collective-permute-done.71), channel_id=1, source_target_pairs={{0,1},{1,2},{2,3},{3,4},{4,5},{5,6},{6,7},{7,8},{8,9},{9,10},{10,1... | collective-permute-start | bytes 1572872 | tf_op jit(solution)/shard_map/ppermute | solution.py:55
  475.7 272.9 %collective-permute-start.92 = (bf16[256,8,128]{0,2,1:T(8,128)(2,1)}, bf16[256,8,128]{0,2,1:T(8,128)(2,1)}, u32[]{:S(2)}, u32[]{:S(2)}) collective-permute-start(bf16[256,8,128]{0,2,1:T(8,128)(2,1)} %collective-permute-done.89), channel_id=1, source_target_pairs={{0,1},{1,2},{2,3},{3,4},{4,5},{5,6},{6,7},{7,8},{8,9},{9,10},{10,1... | collective-permute-start | bytes 1572872 | tf_op jit(solution)/shard_map/ppermute | solution.py:55
  (186 other events, 2414.4 us)
where the time goes:
time: 803 us; the launch traced here: 793 us
  waiting for transfers between devices  332 us (41%)
  matrix products  312 us (39%)
  other arithmetic  136 us (17%)
    ppermute x31, waiting for transfers between devices, local(): sb = lax.ppermute(sb, 'cp', perm)  182 us
    dot_general x32, matrix products, _block(): jnp.einsum('hgqk,khd->qhgd', p.astype(jnp.bfloat16), v, preferred_element...  180 us
    reduce_sum x32, other arithmetic, _block(): l = l * corr + p.sum(axis=-1)  129 us
    dot_general x32, matrix products, _block(): jnp.einsum('qhgd,khd->hgqk', q, k, preferred_element_type=jnp.float32)  105 us
    ppermute x31, waiting for transfers between devices, local(): kb = lax.ppermute(kb, 'cp', perm)  81.5 us
    ppermute x31, waiting for transfers between devices, local(): vb = lax.ppermute(vb, 'cp', perm)  68.1 us
  transfers between devices with their start and end apart: 93, of which 75 were waited for; matrix products, arithmetic and copies ran while one was open for 52% of the time, Pallas kernels for 0%

commit v1 on v0

v1 whole, which is shorter than its diff:
```python
import functools
import math

import jax
import jax.numpy as jnp
from jax import lax
from jax.experimental import pallas as pl
from jax.experimental.pallas import tpu as pltpu
from jax.sharding import PartitionSpec as P

DH = 128
PC = 128
KB = 4
MESH = pl.DeviceIdType.MESH
NEG_INF = float("-inf")
FLOOR = -3e38


class Place:
    def __init__(self, n):
        me = lax.axis_index("cp")
        self.n, self.side = n, math.isqrt(n // 2)
        self.me = me
        self.c = lax.rem(me, 2)
        chip = me // 2
        self.x = lax.rem(chip, self.side)
        self.y = chip // self.side
        self.xin = self.x + 1 - 2 * lax.rem(self.x, 2)
        self.xcross = self.side - 1 - self.x
        self.px = lax.rem(lax.rem(self.x, 2) + self.x // 2, 2)

    def dev(self, x, y, c):
        return (y * self.side + x) * 2 + c

    def row(self, dy):
        return lax.rem(self.y + dy + self.side, self.side)

    def col(self, dx):
        return self.xin if dx else self.x

    def peer(self, dx, dy):
        return self.dev(self.col(dx), self.row(dy), self.c)

    def head(self, dx, dy):
        return lax.rem(self.px + dx, 2) * self.side + self.row(dy)

    def slot(self, dx, dy):
        return self.row(dy) * 2 + lax.rem(self.x + dx, 2)


class Pairs:
    def __init__(self, pt, n, g, scale, first_of, seg_v, pieces, kv, q, t_sc, acc_sc):
        self.pt, self.n, self.g, self.scale, self.first_of, self.seg_v = pt, n, g, scale, first_of, seg_v
        self.pieces, self.kv, self.q, self.t_sc, self.acc_sc = pieces, kv, q, t_sc, acc_sc

    def begins(self, row, half):
        out = []
        for u in range(2):
            src = self.pt.dev((self.pt.x // 2) * 2 + u, row, self.pt.c)
            before = jnp.where(self.seg_v[...] < self.first_of(src, half), 1.0, 0.0)
            out.append(jnp.sum(before).astype(jnp.int32))
        return out

    def __call__(self, row, half, lo, begins, store):
        pt, n, g, scale, seg_v, kv = self.pt, self.n, self.g, self.scale, self.seg_v, self.kv
        t_sc, acc_sc = self.t_sc, self.acc_sc
        last_piece, pieces = 2 * n - 1, self.pieces
        srcs = [pt.dev((pt.x // 2) * 2 + u, row, pt.c) for u in range(2)]
        ps = [last_piece - src if half else src for src in srcs]
        end = jnp.maximum(ps[0], ps[1])
        wide = g * PC
        acc_sc[...] = jnp.zeros_like(acc_sc)

        def queries(us):
            return jnp.concatenate([self.q(row, u, w) for u in us for w in range(g)], axis=1)

        def start(b):
            return jnp.minimum(lo + b * KB, pieces - KB)

        def scores(b):
            j0, js = lo + b * KB, start(b)
            k = jnp.concatenate([kv(js + w, 0) for w in range(KB)], axis=0)
            s = jnp.dot(k, queries((0, 1)), preferred_element_type=jnp.float32)
            pos = lax.broadcasted_iota(jnp.int32, (KB * PC, DH), 0) + js * PC
            tops = []
            for u in range(2):
                seen = (pos >= jnp.maximum(begins[u], j0 * PC)) & (pos < ps[u] * PC)
                for w in range(g):
                    at = slice(u * wide + w * PC, u * wide + (w + 1) * PC)
                    part = jnp.where(seen, s[:, at], NEG_INF)
                    t_sc[:, at] = part
                    tops.append(jnp.max(part, axis=0, keepdims=True))
            return jnp.concatenate(tops, axis=1)

        def step(b, carry):
            m, l, top = carry
            js = start(b)
            m_new = jnp.maximum(m, top)
            corr = jnp.exp2((m - m_new) * scale)
            p = jnp.exp2((t_sc[...] - m_new) * scale)
            l = l * corr + jnp.sum(p, axis=0, keepdims=True)
            vt = jnp.concatenate([kv(js + w, 1) for w in range(KB)], axis=1)
            acc_sc[...] = acc_sc[...] * corr + jnp.dot(vt, p.astype(jnp.bfloat16), preferred_element_type=jnp.float32)
            return m_new, l, scores(b + 1)

        line = jnp.zeros((1, 2 * wide), jnp.float32)
        m, l, _ = lax.fori_loop(0, lax.div(end - lo + KB - 1, KB), step, (line + FLOOR, line, scores(0)))

        key = lax.broadcasted_iota(jnp.int32, (PC, PC), 0)
        query = lax.broadcasted_iota(jnp.int32, (PC, PC), 1)
        ss = [jnp.dot(kv(ps[u], 0), queries((u,)), preferred_element_type=jnp.float32) for u in range(2)]
        for u in range(2):
            at = slice(u * wide, (u + 1) * wide)
            ids = seg_v[srcs[u], pl.ds(half, 1), :]
            idb = jnp.broadcast_to(ids, (PC, PC))
            allowed = jnp.concatenate([(idb == jnp.transpose(idb)) & (key <= query)] * g, axis=1)
            keep = jnp.concatenate([ids == self.first_of(srcs[u], half)] * g, axis=1)
            s = jnp.where(allowed, ss[u], NEG_INF)
            m_old = jnp.where(keep, m[:, at], FLOOR)
            m_new = jnp.maximum(m_old, jnp.max(s, axis=0, keepdims=True))
            corr = jnp.where(keep, jnp.exp2((m_old - m_new) * scale), 0.0)
            p = jnp.exp2((s - m_new) * scale)
            ll = l[:, at] * corr + jnp.sum(p, axis=0, keepdims=True)
            acc = acc_sc[:, at] * corr + jnp.dot(kv(ps[u], 1), p.astype(jnp.bfloat16), preferred_element_type=jnp.float32)
            o = acc * (1.0 / ll)
            for w in range(g):
                store(u, w, jnp.transpose(o[:, w * PC:(w + 1) * PC]).astype(jnp.bfloat16))


def _pair_scratch(g):
    f32 = jnp.float32
    return [pltpu.VMEM((KB * PC, 2 * g * PC), f32), pltpu.VMEM((DH, 2 * g * PC), f32)]


FAR = 2
KV_ORDER = (FAR, 0, 1, -1)
Q_ORDER = (FAR, 1, -1, 0)
O_ORDER = (0, 1, -1, FAR)


def _project(n, g, scale, x_ref, seg_in, wk, wv, wq, kv_o, q_o, segs_o, o_o, wkvb, wqb, kvacc, qacc, kvb, qb, skv, sq, rkv, rq,
             segb, seg_s, ol, t_sc, acc_sc, wkv_sem, wq_sem, kv_send, kv_recv, rkv_recv, rkv_send, fx_send, fs_send,
             q_send, q_recv, rq_recv, rq_send, seg_send, seg_recv, seg_sem, out_sem, qout_sem, o_sem):
    pt = Place(n)
    me = pt.me
    ng = qb.shape[0]
    kv_steps = [(t, dx, dy) for t, dy in enumerate(KV_ORDER) for dx in range(2)]
    q_steps = [(t, dx, dy) for t, dy in enumerate(Q_ORDER) for dx in range(2)]
    own_kv = (KV_ORDER.index(0), 0)
    own_q = (Q_ORDER.index(0), 0)
    gd = g * DH
    kr = wqb.shape[1]
    nk = wqb.shape[0]
    my_head, my_slot = pt.head(0, 0), pt.slot(0, 0)

    kv_copies = [[pltpu.make_async_copy(w.at[pl.ds(t * kr, kr)], wkvb.at[i, t], wkv_sem.at[i, t]) for i, w in enumerate((wk, wv))]
                 for t in range(nk)]
    q_copies = [pltpu.make_async_copy(wq.at[pl.ds(t * kr, kr)], wqb.at[t], wq_sem.at[t]) for t in range(nk)]
    for cps in kv_copies:
        for cp in cps:
            cp.start()
    for cp in q_copies:
        cp.start()

    barrier = pltpu.get_barrier_semaphore()

    @pl.loop(1, n)
    def _(i):
        pl.semaphore_signal(barrier, inc=1, device_id={"cp": lax.rem(me + i, n)}, device_id_type=MESH)

    def put(src, dst, send, recv, dev):
        return pltpu.make_async_remote_copy(src, dst, send, recv, device_id={"cp": dev}, device_id_type=MESH)

    def seg_copy(i):
        return put(seg_in, segb.at[pl.ds(me, 1)], seg_send.at[i], seg_recv.at[me], lax.rem(me + i, n))

    seg_own = pltpu.make_async_copy(seg_in, segb.at[pl.ds(me, 1)], seg_sem.at[0])
    seg_own.start()

    way = (1, -1)

    def kv_copy(half, t, dx, dy):
        return put(skv.at[pt.head(dx, dy), half], kvb.at[me, half], kv_send.at[half, 2 * t + dx], kv_recv.at[half, me],
                   pt.peer(dx, dy))

    def kv_hop(half, dx):
        return put(skv.at[pt.head(dx, FAR), half], rkv.at[half, dx], kv_send.at[half, dx], rkv_recv.at[half, dx],
                   pt.peer(0, way[half]))

    def kv_hand(half, dx):
        src = pt.peer(0, -way[half])
        return put(rkv.at[half, dx], kvb.at[src, half], rkv_send.at[half, dx], kv_recv.at[half, src], pt.peer(dx, way[half]))

    def q_copy(half, t, dx, dy):
        return put(sq.at[pt.head(dx, dy), half], qb.at[my_slot, half], q_send.at[half, 2 * t + dx], q_recv.at[half, my_slot],
                   pt.peer(dx, dy))

    def q_hop(half, dx):
        return put(sq.at[pt.head(dx, FAR), half], rq.at[half, dx], q_send.at[half, dx], rq_recv.at[half, dx],
                   pt.peer(0, way[half]))

    def q_hand(half, dx):
        slot = pt.slot(0, -way[half])
        return put(rq.at[half, dx], qb.at[slot, half], rq_send.at[half, dx], q_recv.at[half, slot], pt.peer(dx, way[half]))

    nb = 4 * DH

    def summed(t, w, acc, c):
        cols = slice(c * nb, (c + 1) * nb)
        r = jnp.dot(x_ref[:, t * kr:(t + 1) * kr], w[:, cols], preferred_element_type=jnp.float32)
        if t > 0:
            r = r + acc[:, cols]
        if t < nk - 1:
            acc[:, cols] = r
        return r

    def kv_step(t):
        for cp in kv_copies[t]:
            cp.wait()
        for c in range(wkvb.shape[3] // nb):
            for i in range(2):
                r = summed(t, wkvb.at[i, t], kvacc.at[i], c)
                if t == nk - 1:
                    for u in range(nb // DH):
                        part = r[:, u * DH:(u + 1) * DH]
                        part = (jnp.transpose(part) if i == 1 else part).astype(jnp.bfloat16)
                        for half in range(2):
                            rows = slice(half * PC, (half + 1) * PC)
                            skv[c * (nb // DH) + u, half, i] = part[:, rows] if i == 1 else part[rows]

    def q_step(t, first, last):
        if first == 0:
            q_copies[t].wait()
        for c in range(first, last):
            r = summed(t, wqb.at[t], qacc, c)
            if t == nk - 1:
                for u in range(nb // DH):
                    col = c * (nb // DH) + u
                    part = jnp.transpose(r[:, u * DH:(u + 1) * DH]).astype(jnp.bfloat16)
                    for half in range(2):
                        sq[col // g, half, col % g] = part[:, half * PC:(half + 1) * PC]

    def send_kv(half):
        for dx in range(2):
            kv_hop(half, dx).start()
        for t, dx, dy in kv_steps:
            if dy != FAR and (t, dx) != own_kv:
                kv_copy(half, t, dx, dy).start()

    def send_q(half):
        for dx in range(2):
            q_hop(half, dx).start()
        for t, dx, dy in q_steps:
            if dy != FAR and (t, dx) != own_q:
                q_copy(half, t, dx, dy).start()

    def hand_on(half, kind):
        buf, recv, hand = (rkv, rkv_recv, kv_hand) if kind == "kv" else (rq, rq_recv, q_hand)
        for dx in range(2):
            put(buf.at[half, dx], buf.at[half, dx], kv_send.at[0, 0], recv.at[half, dx], me).wait_recv()
            hand(half, dx).start()

    def to_cross(half, src, i):
        return put(kvb.at[src, half], kvb.at[src, half], fx_send.at[half, i], kv_recv.at[half, src], pt.dev(pt.xcross, pt.y, pt.c))

    def to_sibling(half, src, i):
        return put(kvb.at[src, half], kvb.at[src, half], fs_send.at[half, i], kv_recv.at[half, src], pt.dev(pt.x, pt.y, 1 - pt.c))

    def kv_out(half, src):
        return pltpu.make_async_copy(kvb.at[src, half], kv_o.at[src, half], out_sem.at[half, src])

    def q_out(slot):
        return pltpu.make_async_copy(qb.at[slot, 1], q_o.at[slot], qout_sem.at[slot])

    def arrived(half, src):
        to_sibling(half, src, 0).wait_recv()

    def forward(half, t, dxs=(0, 1)):
        for dx in dxs:
            src = pt.peer(dx, -KV_ORDER[t])
            if (t, dx) != own_kv:
                arrived(half, src)
            to_cross(half, src, 2 * t + dx).start()
            to_sibling(half, src, 2 * t + dx).start()
            kv_out(half, src).start()

    def mirrored(dx, dy, c):
        return pt.dev(pt.side - 1 - pt.col(dx), pt.row(-dy), c)

    own_t = own_kv[0]
    passing = [(t, dx, KV_ORDER[t]) for t in (1, 2, 3, 0) for dx in range(2)]

    def pass_on(half, steps):
        for t, dx, dy in steps:
            src = mirrored(dx, dy, pt.c)
            arrived(half, src)
            to_sibling(half, src, 8 + 2 * t + dx).start()
            kv_out(half, src).start()

    def from_sibling(half):
        for far_side in range(2):
            for t, dx, dy in passing:
                src = mirrored(dx, dy, 1 - pt.c) if far_side else pt.dev(pt.col(dx), pt.row(-dy), 1 - pt.c)
                arrived(half, src)
                kv_out(half, src).start()

    def queries(half):
        for t, dx, dy in q_steps:
            slot = pt.slot(dx, -dy)
            if (t, dx) != own_q:
                put(qb.at[slot, half], qb.at[slot, half], q_send.at[0, 0], q_recv.at[half, slot], me).wait_recv()
            if half:
                q_out(slot).start()

    for t in range(nk):
        kv_step(t)
    kvb[me] = skv[my_head]
    nq = wqb.shape[2] // nb
    q_step(0, 0, 1)

    pl.semaphore_wait(barrier, n - 1)
    send_kv(0)
    forward(0, own_t, (0,))
    forward(1, own_t, (0,))

    @pl.loop(1, n)
    def _(i):
        seg_copy(i).start()

    q_step(0, 1, nq)
    q_step(1, 0, nq)
    q_step(2, 0, nq)
    forward(0, own_t, (1,))
    hand_on(0, "kv")
    q_step(3, 0, nq)
    qb[my_slot] = sq[my_head]
    forward(0, 2)
    send_q(0)
    send_kv(1)
    send_q(1)
    forward(0, 3)
    forward(0, 0)
    pass_on(0, passing[:4])
    hand_on(0, "q")
    pass_on(0, passing[4:])
    from_sibling(0)
    queries(0)
    seg_own.wait()

    @pl.loop(1, n)
    def _(i):
        src = lax.rem(me + i, n)
        put(seg_in, segb.at[pl.ds(src, 1)], seg_send.at[i], seg_recv.at[src], src).wait_recv()

    seg_copies = [pltpu.make_async_copy(segb, seg_s, seg_sem.at[1]), pltpu.make_async_copy(segb, segs_o, seg_sem.at[2])]
    for cp in seg_copies:
        cp.start()
    for cp in seg_copies:
        cp.wait()

    pairs = Pairs(pt, n, g, scale, lambda src, half: seg_s[src, half, 0], segb, n, lambda p, i: kvb[p, 0, i],
                  lambda row, u, w: qb[2 * row + u, 0, w], t_sc, acc_sc)

    def o_out(row):
        return pltpu.make_async_copy(ol.at[pl.ds(2 * row, 2)], o_o.at[pl.ds(2 * row, 2)], o_sem.at[row])

    def low(row, carry):
        def store(u, w, val):
            ol[2 * row + u, :, w * DH:(w + 1) * DH] = val

        pairs(row, 0, 0, pairs.begins(row, 0), store)

        @pl.when(row == 0)
        def _():
            forward(1, own_t, (1,))
            hand_on(1, "kv")
            forward(1, 2)

        @pl.when(row == 1)
        def _():
            forward(1, 3)
            o_out(0).start()

        @pl.when(row == 2)
        def _():
            forward(1, 0)
            hand_on(1, "q")
            pass_on(1, passing[:4])
            o_out(1).start()

        return carry

    lax.fori_loop(0, ng // 2, low, 0)
    pass_on(1, passing[4:])
    o_out(2).start()
    from_sibling(1)
    queries(1)
    o_out(3).start()

    @pl.loop(1, n)
    def _(i):
        seg_copy(i).wait_send()

    for half in range(2):
        for dx in range(2):
            kv_hop(half, dx).wait_send()
            kv_hand(half, dx).wait_send()
            q_hop(half, dx).wait_send()
            q_hand(half, dx).wait_send()
        for t, dx, dy in kv_steps:
            if dy != FAR and (t, dx) != own_kv:
                kv_copy(half, t, dx, dy).wait_send()
            src = pt.peer(dx, -dy)
            to_cross(half, src, 2 * t + dx).wait_send()
            to_sibling(half, src, 2 * t + dx).wait_send()
            to_sibling(half, src, 8 + 2 * t + dx).wait_send()
        for t, dx, dy in q_steps:
            if dy != FAR and (t, dx) != own_q:
                q_copy(half, t, dx, dy).wait_send()

        @pl.loop(0, n)
        def _(i):
            kv_out(half, i).wait()

    for i in range(ng):
        q_out(i).wait()
    for row in range(ng // 2):
        o_out(row).wait()


def _attend(n, g, scale, segs, kv, q_in, o_out, seg_s, seg_v, kvs, qs, os, lo_s, t_sc, acc_sc,
            seg_sem, kv_sem, q_sem, o_sem):
    pt = Place(n)
    last_piece = 2 * n - 1
    ng = q_in.shape[0]

    def load(p):
        owner = jnp.where(p < n, p, last_piece - p)
        return pltpu.make_async_copy(kv.at[owner, jnp.where(p < n, 0, 1)], kvs.at[p], kv_sem)

    seg_copies = [pltpu.make_async_copy(segs, seg_v, seg_sem.at[0]), pltpu.make_async_copy(segs, seg_s, seg_sem.at[1])]
    q_copies = [pltpu.make_async_copy(q_in.at[i], qs.at[i], q_sem) for i in range(ng)]
    for cp in seg_copies + q_copies:
        cp.start()

    @pl.loop(0, 2 * n)
    def _(p):
        load(p).start()

    for cp in seg_copies:
        cp.wait()
    pairs = Pairs(pt, n, g, scale, lambda src, half: seg_s[src, half, 0], seg_v, 2 * n, lambda p, i: kvs[p, i],
                  lambda row, u, w: qs[2 * row + u, w], t_sc, acc_sc)
    for i in range(ng // 2):
        for u, at in enumerate(pairs.begins(i, 1)):
            lo_s[2 * i + u] = at
    for cp in q_copies:
        cp.wait()

    @pl.loop(0, 2 * n)
    def _(p):
        load(p).wait()

    def out(slot):
        return pltpu.make_async_copy(os.at[slot], o_out.at[slot], o_sem)

    def one(row, carry):
        def store(u, w, val):
            os[2 * row + u, :, w * DH:(w + 1) * DH] = val

        begins = [lo_s[2 * row + u] for u in range(2)]
        pairs(row, 1, lax.div(jnp.minimum(*begins), PC), begins, store)

        @pl.when(row > 0)
        def _():
            for u in range(2):
                out(2 * (row - 1) + u).start()

        return carry

    lax.fori_loop(0, ng // 2, one, 0)
    for u in range(2):
        out(ng - 2 + u).start()
    for i in range(ng):
        out(i).wait()


def _combine(n, g, o_lo, o_hi, wo, y_ref, obuf, robuf, wob, acc, w_sem, o_send, o_recv, ro_recv, ro_send):
    pt = Place(n)
    me = pt.me
    gd = g * DH
    my_head, my_slot = pt.head(0, 0), pt.slot(0, 0)
    nc = 4
    wn = y_ref.shape[1] // nc
    rows = (pl.ds(0, PC), pl.ds(PC, PC))
    parts = (o_lo, o_hi)

    own = [pltpu.make_async_copy(parts[half].at[my_slot], obuf.at[my_head, rows[half]], o_recv.at[half, my_head]) for half in range(2)]
    for cp in own:
        cp.start()

    def w_copies(t):
        for dx in range(2):
            h = pl.multiple_of(pt.head(dx, O_ORDER[t]) * gd, gd)
            yield pltpu.make_async_copy(wo.at[pl.ds(h, gd), :], wob.at[t, pl.ds(dx * gd, gd), :], w_sem.at[t, dx])

    for t in range(len(O_ORDER)):
        for cp in w_copies(t):
            cp.start()

    others = [(dx, dy) for dy in O_ORDER for dx in range(2) if (dx, dy) != (0, 0)]
    near = [s for s in others if s[1] != FAR]
    barrier = pltpu.get_barrier_semaphore()
    for dx, dy in others:
        pl.semaphore_signal(barrier, inc=1, device_id={"cp": pt.peer(dx, dy)}, device_id_type=MESH)
    pl.semaphore_wait(barrier, len(others))

    def put(src, dst, send, recv, dev):
        return pltpu.make_async_remote_copy(src, dst, send, recv, device_id={"cp": dev}, device_id_type=MESH)

    way = (1, -1)

    def o_copy(half, i):
        dx, dy = near[i]
        return put(parts[half].at[pt.slot(dx, dy)], obuf.at[my_head, rows[half]], o_send.at[half, i], o_recv.at[half, my_head],
                   pt.peer(dx, dy))

    def o_hop(half, dx):
        return put(parts[half].at[pt.slot(dx, FAR)], robuf.at[half, dx], o_send.at[half, len(near) + dx], ro_recv.at[half, dx],
                   pt.peer(0, way[half]))

    def o_hand(half, dx):
        head = pt.head(0, -way[half])
        return put(robuf.at[half, dx], obuf.at[head, rows[half]], ro_send.at[half, dx], o_recv.at[half, head],
                   pt.peer(dx, way[half]))

    def hand_on(half):
        for dx in range(2):
            put(robuf.at[half, dx], robuf.at[half, dx], o_send.at[0, 0], ro_recv.at[half, dx], me).wait_recv()
            o_hand(half, dx).start()

    for half in range(2):
        o_copy(half, 0).start()
        for dx in range(2):
            o_hop(half, dx).start()
    for half in range(2):
        for i in range(1, len(near)):
            o_copy(half, i).start()

    for t, dy in enumerate(O_ORDER):
        for cp in w_copies(t):
            cp.wait()
        heads = [pt.head(dx, dy) for dx in range(2)]
        for dx in range(2):
            for half in range(2):
                if dy == 0 and dx == 0:
                    own[half].wait()
                else:
                    put(robuf.at[0, 0], obuf.at[heads[dx], rows[half]], o_send.at[0, 0], o_recv.at[half, heads[dx]], me).wait_recv()
        a = jnp.concatenate([obuf[heads[0]], obuf[heads[1]]], axis=1)
        for u in range(nc):
            r = jnp.dot(a, wob[t, :, u * wn:(u + 1) * wn], preferred_element_type=jnp.float32)
            if t > 0:
                r = r + acc[:, u * wn:(u + 1) * wn]
            if t < len(O_ORDER) - 1:
                acc[:, u * wn:(u + 1) * wn] = r
            else:
                y_ref[:, u * wn:(u + 1) * wn] = r.astype(y_ref.dtype)
        if t == 0:
            for half in range(2):
                hand_on(half)
    for half in range(2):
        for i in range(len(near)):
            o_copy(half, i).wait_send()
        for dx in range(2):
            o_hop(half, dx).wait_send()
            o_hand(half, dx).wait_send()


def solution(mesh):
    n = mesh.shape["cp"]
    side = math.isqrt(n // 2)
    bf, f32 = jnp.bfloat16, jnp.float32
    vmem, anym = pl.BlockSpec(memory_space=pltpu.VMEM), pl.BlockSpec(memory_space=pltpu.HBM)
    dma = pltpu.SemaphoreType.DMA

    def local(x, seg, wq, wk, wv, wo):
        lq, d = x.shape
        hkv = wk.shape[1] // DH
        g = wq.shape[1] // wk.shape[1]
        gd = g * DH
        ng = 2 * side
        scale = DH ** -0.5 * math.log2(math.e)
        i32 = jnp.int32
        o_part = jax.ShapeDtypeStruct((ng, PC, gd), bf)
        kv, q, segs, o_lo = pl.pallas_call(
            functools.partial(_project, n, g, scale),
            out_shape=(jax.ShapeDtypeStruct((n, 2, 2, PC, DH), bf), jax.ShapeDtypeStruct((ng, g, PC, DH), bf),
                       jax.ShapeDtypeStruct((n, 2, PC), i32), o_part),
            in_specs=[vmem, anym, anym, anym, anym],
            out_specs=(anym,) * 4,
            scratch_shapes=[
                pltpu.VMEM((2, side, d // side, hkv * DH), bf), pltpu.VMEM((side, d // side, hkv * gd), bf),
                pltpu.VMEM((2, lq, hkv * DH), f32), pltpu.VMEM((lq, hkv * gd), f32),
                pltpu.VMEM((n, 2, 2, PC, DH), bf), pltpu.VMEM((ng, 2, g, PC, DH), bf),
                pltpu.VMEM((ng, 2, 2, PC, DH), bf), pltpu.VMEM((ng, 2, g, PC, DH), bf),
                pltpu.VMEM((2, 2, 2, PC, DH), bf), pltpu.VMEM((2, 2, g, PC, DH), bf),
                pltpu.VMEM((n, 2, PC), i32), pltpu.SMEM((n, 2, PC), i32), pltpu.VMEM((ng, PC, gd), bf)] + _pair_scratch(g) + [
                dma((2, side)), dma((side,)), dma((2, ng)), dma((2, n)), dma((2, 2)), dma((2, 2)), dma((2, ng)), dma((2, 2 * ng)),
                dma((2, ng)), dma((2, ng)), dma((2, 2)), dma((2, 2)), dma((n,)), dma((n,)), dma((3,)), dma((2, n)), dma((ng,)),
                dma((ng // 2,)),
            ],
            compiler_params=pltpu.CompilerParams(collective_id=0, has_side_effects=True, vmem_limit_bytes=60 << 20),
            name="project",
        )(x, seg.reshape(1, 2, PC), wk, wv, wq)
        o = pl.pallas_call(
            functools.partial(_attend, n, g, scale),
            out_shape=o_part,
            in_specs=[anym] * 3,
            out_specs=anym,
            scratch_shapes=[pltpu.SMEM((n, 2, PC), jnp.int32), pltpu.VMEM((n, 2, PC), jnp.int32),
                            pltpu.VMEM((2 * n, 2, PC, DH), bf), pltpu.VMEM((ng, g, PC, DH), bf),
                            pltpu.VMEM((ng, PC, gd), bf), pltpu.SMEM((ng,), jnp.int32)] + _pair_scratch(g) + [dma((2,)), dma, dma, dma],
            compiler_params=pltpu.CompilerParams(vmem_limit_bytes=60 << 20),
            name="attend",
        )(segs, kv, q)
        return pl.pallas_call(
            functools.partial(_combine, n, g),
            out_shape=jax.ShapeDtypeStruct((lq, wo.shape[1]), bf),
            in_specs=[anym] * 3,
            out_specs=vmem,
            scratch_shapes=[pltpu.VMEM((hkv, lq, gd), bf), pltpu.VMEM((2, 2, PC, gd), bf),
                            pltpu.VMEM((side, 2 * gd, wo.shape[1]), bf), pltpu.VMEM((lq, wo.shape[1]), f32),
                            dma((side, 2)), dma((2, ng)), dma((2, ng)), dma((2, 2)), dma((2, 2))],
            compiler_params=pltpu.CompilerParams(collective_id=1, has_side_effects=True, vmem_limit_bytes=60 << 20),
            name="combine",
        )(o_lo, o, wo)

    rows = P(("dp", "cp"), None)
    return jax.shard_map(local, mesh=mesh, in_specs=(rows, P(("dp", "cp")), P(), P(), P(), P()), out_specs=rows, check_vma=False)
```

time: 803 us -> 110 us (0.14)
  the two profiles are of different devices: /device:TPU:96 before, /device:TPU:100 now
where the time goes in v1:
time: 110 us
  Pallas kernels  107 us (97%)
  local copies, waits for them, and re-layouts  2.65 us (2%)
    pallas_call x1, Pallas kernels, local(): pl.pallas_call(functools.partial(_project, n, g, scale), out_shape=(jax.S...  67.1 us
    pallas_call x1, Pallas kernels, local(): pl.pallas_call(functools.partial(_combine, n, g), out_shape=jax.ShapeDtyp...  25.5 us
    pallas_call x1, Pallas kernels, local(): pl.pallas_call(functools.partial(_attend, n, g, scale), out_shape=o_part,...  14.5 us
    unnamed x1, local copies, waits for them, and re-layouts  2.65 us

profile of v1, /device:TPU:100, one launch (start us, length us, event | category | flops | bytes accessed | tf_op | source)
XLA Modules:
  0.0 109.8 jit_solution(4633071388851780880)
XLA Ops:
  0.0 67.1 %project.1 = (bf16[32,2,2,128,128]{4,3,2,1,0:T(8,128)(2,1)}, bf16[8,3,128,128]{3,2,1,0:T(8,128)(2,1)}, s32[32,2,128]{2,1,0:T(2,128)}, bf16[8,128,384]{2,1,0:T(8,128)(2,1)}) custom-call(bf16[256,3072]{1,0:T(8,128)(2,1)} %x_ref.1, s32[1,2,128]{2,1,0:T(2,128)} %bitcast.1, bf16[3072,1024]{1,0:T(8,128)(2,1)} %wk.1, bf16[3072,1024]{1,0:T(8,128)(2,1)} %wv.1, ...), custom_call_target="tpu_custom_call" | custom-call | tf_op jit(solution)/shard_map/project/pallas_call | solution.py:596
  67.1 14.5 %attend.1.o_hi = bf16[8,128,384]{2,1,0:T(8,128)(2,1)} custom-call(s32[32,2,128]{2,1,0:T(2,128)} %get-tuple-element.10.segs, bf16[32,2,2,128,128]{4,3,2,1,0:T(8,128)(2,1)} %get-tuple-element.11.kv, bf16[8,3,128,128]{3,2,1,0:T(8,128)(2,1)} %get-tuple-element.12.q_in), custom_call_target="tpu_custom_call" | custom-call | tf_op jit(solution)/shard_map/attend/pallas_call | solution.py:616
  81.6 25.5 %combine.1 = bf16[256,3072]{1,0:T(8,128)(2,1)} custom-call(bf16[8,128,384]{2,1,0:T(8,128)(2,1)} %get-tuple-element.9.o_lo, bf16[8,128,384]{2,1,0:T(8,128)(2,1)} %attend.1.o_hi, bf16[3072,3072]{1,0:T(8,128)(2,1)} %wo.1), custom_call_target="tpu_custom_call" | custom-call | tf_op jit(solution)/shard_map/combine/pallas_call | solution.py:627
  107.2 2.7 %copy.8 = bf16[256,3072]{1,0:T(8,128)(2,1)} copy(bf16[256,3072]{1,0:T(8,128)(2,1)} %combine.1) | data formatting | bytes 3145728
